TPU v7x, 128 devices: a whole 4x4x4 slice. The times are simulated.
128 devices in a mesh: area: 32 (over z, y, core), local: 4 (over x).
Axes of the slice: x: 4, y: 4, z: 4, core: 2. Of those that a mesh axis runs over, the one named last changes fastest.
Arguments:
- potential: float32 [8, 524288], P(None, ('area', 'local')), may hold values from -6 to 6
- current: float32 [8, 524288], P(None, ('area', 'local')), may hold values from -4 to 4
- ext_drive: float32 [8, 524288], P(None, ('area', 'local')), may hold values from -6 to 6
- decay_syn: float32 [524288], P(('area', 'local')), may hold values from 0.3 to 0.97
- decay_mem: float32 [524288], P(('area', 'local')), may hold values from 0.4 to 0.95
- weights: bfloat16 [128, 128, 2, 128, 128], P(('area', 'local')), may hold values from -0.25 to 0.25
- tile_src: int32 [128, 128, 2], P(('area', 'local')), may hold values from 0 to 31
- tile_dst: int32 [128, 128, 2], P(('area', 'local')), may hold values from 0 to 31
- blk_pop: int32 [4096], P(('area', 'local')), may hold values from 0 to 7
- tile_route: int32 [5, 128, 128, 1], P(None, ('area', 'local')), may hold values from 0 to 1, as said below
- counts: int32 [5, 128, 128], P(None, ('area', 'local')), may hold values from 0 to 1, as said below
Outputs:
- volts_out: float32 [8, 524288], P(None, ('area', 'local'))
- current_out: float32 [8, 524288], P(None, ('area', 'local'))
- pop_rates: float32 [32, 5, 8, 8], P('area')
Inputs may be any that keep to these rules, and one draw needn't show every extreme that they name: `tile_route`: the 1 entries of one list name distinct tiles; entries at and beyond counts of that list are unused. `counts`: in every step some target device gets 1 tiles from every sending device.
All inputs are finite; a program needn't handle non-finite values.
Results may differ from a plain program's by a relative error of at most 0.0029.
Values may be sent and summed in bfloat16 or wider, within the bound.
No kernel may reach another device: no remote copies, remote signals or barrier semaphores. Data moves between devices by JAX's collectives and lax.ppermute only.
A program may use at most 64 MiB of HBM per device.

v0:
```python
import jax
import jax.numpy as jnp
from jax import lax
from jax.sharding import PartitionSpec as P

POPS = 8
spike_gain = 4.0
threshold = 1.0
reset_size = 0.5


def from_everyone(array, axis):
    copies = jnp.broadcast_to(array, (lax.axis_size(axis), *array.shape))
    return lax.all_to_all(copies, axis, split_axis=0, concat_axis=0, tiled=True)


def of_everyone(array, axis):
    return from_everyone(array, axis).sum(axis=0)


def shards(
    potential,
    current,
    ext_drive,
    decay_syn,
    decay_mem,
    weights,
    tile_src,
    tile_dst,
    blk_pop,
    tile_route,
    counts,
):
    dev_count = weights.shape[1]
    tile_count = weights.shape[2]
    block_width = weights.shape[3]
    blk_count = blk_pop.shape[0]
    trial_count = potential.shape[0]
    slot_count = tile_route.shape[3]
    step_count = tile_route.shape[0]
    tile_table = weights[0]
    routes = tile_route[:, 0]
    slot_valid = jnp.arange(slot_count, dtype=jnp.int32)[None, None, :] < counts[:, 0][:, :, None]
    table_shape = (step_count, dev_count, tile_count)
    src_blocks = jnp.take_along_axis(
        jnp.broadcast_to(tile_src[0][None], table_shape), routes, axis=2
    )
    dst_blocks = jnp.take_along_axis(
        jnp.broadcast_to(tile_dst[0][None], table_shape), routes, axis=2
    )
    dst_ids = jnp.where(slot_valid, dst_blocks, -1)
    arrived_ids = lax.all_to_all(
        dst_ids, ("area", "local"), split_axis=1, concat_axis=1, tiled=True
    )
    state_shape = (trial_count, blk_count, block_width)
    volts = potential.reshape(state_shape)
    syn_cur = current.reshape(state_shape)
    ext_field = ext_drive.reshape(state_shape)
    syn_decay = decay_syn.reshape((1, blk_count, block_width))
    mem_decay = decay_mem.reshape((1, blk_count, block_width))
    pop_table = (blk_pop[:, None] == jnp.arange(POPS, dtype=jnp.int32)[None, :]).astype(jnp.float32)
    block_ids = jnp.arange(blk_count, dtype=jnp.int32)

    def advance(step_idx, state_now):
        volts, syn_cur, rate_acc = state_now
        spikes = jax.nn.sigmoid(spike_gain * (volts - threshold))
        spike_blocks = jnp.transpose(spikes.astype(jnp.bfloat16), (1, 0, 2))
        activity = jnp.sum(spikes, axis=2)
        rate_now = jnp.dot(activity, pop_table, precision=lax.Precision.HIGHEST)
        rate_acc = lax.dynamic_update_index_in_dim(rate_acc, rate_now, step_idx, 0)
        chosen = routes[step_idx]
        picked = jnp.take_along_axis(tile_table, chosen[:, :, None, None], axis=1)
        senders = jnp.take(spike_blocks, src_blocks[step_idx], axis=0)
        outgoing = jnp.einsum(
            "tcrn,tcnm->tcrm", senders, picked, preferred_element_type=jnp.float32
        ).astype(jnp.bfloat16)
        arrived = lax.all_to_all(
            outgoing, ("area", "local"), split_axis=0, concat_axis=0, tiled=True
        )
        targets = arrived_ids[step_idx].reshape((dev_count * slot_count,))
        deliver = (targets[:, None] == block_ids[None, :]).astype(jnp.bfloat16)
        inflow = jnp.einsum(
            "sb,srn->rbn",
            deliver,
            arrived.reshape((dev_count * slot_count, trial_count, block_width)),
            preferred_element_type=jnp.float32,
        )
        syn_cur = syn_decay * syn_cur + inflow
        volts = mem_decay * volts + (1.0 - mem_decay) * (syn_cur + ext_field) - reset_size * spikes
        return (volts, syn_cur, rate_acc)

    rate_start = jnp.zeros((step_count, trial_count, POPS), jnp.float32)
    volts, syn_cur, rate_acc = lax.fori_loop(0, step_count, advance, (volts, syn_cur, rate_start))
    totals = of_everyone(rate_acc, "local") / (block_width * blk_count)
    return (volts.reshape((trial_count, -1)), syn_cur.reshape((trial_count, -1)), totals[None])


def solution(mesh):
    in_specs = (
        P(None, ("area", "local")),
        P(None, ("area", "local")),
        P(None, ("area", "local")),
        P(("area", "local")),
        P(("area", "local")),
        P(("area", "local"), None, None, None, None),
        P(("area", "local"), None, None),
        P(("area", "local"), None, None),
        P(("area", "local")),
        P(None, ("area", "local"), None, None),
        P(None, ("area", "local"), None),
    )
    out_specs = (
        P(None, ("area", "local")),
        P(None, ("area", "local")),
        P("area", None, None, None),
    )
    return jax.shard_map(shards, mesh=mesh, in_specs=in_specs, out_specs=out_specs, check_vma=False)
```

profile of v0, /device:TPU:0, one launch (start us, length us, event | category | flops | bytes accessed | tf_op | source)
XLA Modules:
  0.0 181.6 jit_solution(10345220873550262598)
XLA Ops:
  0.6 0.7 fusion.37
  1.4 0.8 copy.54
  2.2 0.0 copy-start.2
  2.3 0.0 copy-start.3
  2.3 0.0 copy-start.7
  2.3 5.6 %gather_fusion.2 = s32[640]{0:T(1024)S(1)} fusion(s32[5,128,2]{2,1,0:T(8,128)S(1)} %broadcast_in_dim.74, s32[640]{0:T(1024)S(1)} %bitcast.118), kind=kCustom, calls=%fused_computation.clone | custom fusion | bytes 12800 | tf_op jit(solution)/shard_map/jit(take_along_axis)/gather | solution.py:45
  8.0 0.1 copy.56
  8.1 5.6 %gather_fusion.3 = s32[640]{0:T(1024)S(1)} fusion(s32[5,128,2]{2,1,0:T(8,128)S(1)} %broadcast_in_dim.76, s32[640]{0:T(1024)S(1)} %bitcast.119), kind=kCustom, calls=%fused_computation.3.clone | custom fusion | bytes 12800 | tf_op jit(solution)/shard_map/jit(take_along_axis)/gather | solution.py:48
  13.8 0.7 copy.58
  14.6 11.2 %all-to-all-start.1 = ((s32[5,128,1]{0,2,1:T(1,128)}), s32[5,128,1]{0,2,1:T(1,128)S(1)}, u32[]{:S(2)}, u32[]{:S(2)}) async-start(s32[5,128,1]{0,2,1:T(1,128)} %copy.58), calls=%async_computation.1 | async-start | bytes 131072 | tf_op jit(solution)/shard_map/all_to_all | solution.py:52
  25.8 0.1 copy_bitcast_fusion.2
  25.9 9.1 %all-to-all-done.1 = s32[5,128,1]{0,2,1:T(1,128)S(1)} async-done(((s32[5,128,1]{0,2,1:T(1,128)}), s32[5,128,1]{0,2,1:T(1,128)S(1)}, u32[]{:S(2)}, u32[]{:S(2)}) %all-to-all-start.1) | async-done | bytes 2592 | tf_op jit(solution)/shard_map/all_to_all | solution.py:52
  35.0 0.1 copy.59
  35.1 0.0 copy-done.8
  35.1 135.4 %while.20 = (s32[]{:T(128)}, f32[8,32,128]{2,1,0:T(8,128)S(1)}, f32[8,32,128]{2,1,0:T(8,128)S(1)}, f32[5,8,8]{2,1,0:T(8,128)S(1)}, f32[1,32,128]{2,1,0:T(8,128)S...) while((s32[]{:T(128)}, f32[8,32,128]{2,1,0:T(8,128)S(1)}, ...), condition=%wide.region_2.0_spmd.clone, body=%wide.region_0.3_spmd.clone.sunk | while | flops 44994944 | bytes 15770289 | solution.py:93
  35.2 0.1 fusion.53
  35.4 0.7 gather_fusion.1
  36.1 6.5 %gather_fusion = bf16[128,128,128]{2,1,0:T(8,128)(2,1)} fusion(bf16[128,2,128,128]{3,2,1,0:T(8,128)(2,1)} %get-tuple-element.546, s32[128]{0:T(128)S(1)} %or_bitcast_fusion.2), kind=kCustom, calls=%fused_computation.2.clone.clone.1 | custom fusion | bytes 8389632 | tf_op jit(solution)/shard_map/while/body/eval_jaxpr/jit(take_along_axis)/gather | solution.py:72
  42.5 4.2 %fusion.55 = bf16[128,1,8,128]{3,2,1,0:T(8,128)(2,1)} fusion(bf16[128,128,128]{2,1,0:T(8,128)(2,1)} %gather_fusion, pred[128]{0:T(512)(128)(4,1)S(1)} %get-tuple-element.506, bf16[128,8,128]{2,1,0:T(8,128)(2,1)S(1)} %gather_fusion.1, pred[128]{0:T(512)(128)(4,1)S(1)} %get-tuple-element.508), kind=kOutput, calls=%fused_computation.11.clone.1 | convolution fusion | flops 35913728 | bytes 4718848 | tf_op jit(solution)/shard_map/while/body/eval_jaxpr/tcrn,tcnm->tcrm/dot_general | solution.py:74
  46.7 4.6 %all-to-all-start = ((bf16[128,1,8,128]{3,2,1,0:T(8,128)(2,1)}), bf16[128,1,8,128]{3,2,1,0:T(8,128)(2,1)S(1)}, u32[]{:S(2)}, u32[]{:S(2)}) async-start(bf16[128,1,8,128]{3,2,1,0:T(8,128)(2,1)} %fusion.55), calls=%async_computation | async-start | bytes 524288 | tf_op jit(solution)/shard_map/while/body/eval_jaxpr/all_to_all | solution.py:77
  51.3 0.2 fusion.56
  51.5 10.4 %all-to-all-done = bf16[128,1,8,128]{3,2,1,0:T(8,128)(2,1)S(1)} async-done(((bf16[128,1,8,128]{3,2,1,0:T(8,128)(2,1)}), bf16[128,1,8,128]{3,2,1,0:T(8,128)(2,1)S(1)}, u32[]{:S(2)}, u32[]{:S(2)}) %all-to-all-start) | async-done | bytes 262176 | tf_op jit(solution)/shard_map/while/body/eval_jaxpr/all_to_all | solution.py:77
  62.0 0.2 multiply_subtract_fusion.2
  62.3 0.1 fusion.53
  62.5 0.7 gather_fusion.1
  63.2 6.5 %gather_fusion = bf16[128,128,128]{2,1,0:T(8,128)(2,1)} fusion(bf16[128,2,128,128]{3,2,1,0:T(8,128)(2,1)} %get-tuple-element.546, s32[128]{0:T(128)S(1)} %or_bitcast_fusion.2), kind=kCustom, calls=%fused_computation.2.clone.clone.1 | custom fusion | bytes 8389632 | tf_op jit(solution)/shard_map/while/body/eval_jaxpr/jit(take_along_axis)/gather | solution.py:72
  69.6 4.2 %fusion.55 = bf16[128,1,8,128]{3,2,1,0:T(8,128)(2,1)} fusion(bf16[128,128,128]{2,1,0:T(8,128)(2,1)} %gather_fusion, pred[128]{0:T(512)(128)(4,1)S(1)} %get-tuple-element.506, bf16[128,8,128]{2,1,0:T(8,128)(2,1)S(1)} %gather_fusion.1, pred[128]{0:T(512)(128)(4,1)S(1)} %get-tuple-element.508), kind=kOutput, calls=%fused_computation.11.clone.1 | convolution fusion | flops 35913728 | bytes 4718848 | tf_op jit(solution)/shard_map/while/body/eval_jaxpr/tcrn,tcnm->tcrm/dot_general | solution.py:74
  73.8 4.6 %all-to-all-start = ((bf16[128,1,8,128]{3,2,1,0:T(8,128)(2,1)}), bf16[128,1,8,128]{3,2,1,0:T(8,128)(2,1)S(1)}, u32[]{:S(2)}, u32[]{:S(2)}) async-start(bf16[128,1,8,128]{3,2,1,0:T(8,128)(2,1)} %fusion.55), calls=%async_computation | async-start | bytes 524288 | tf_op jit(solution)/shard_map/while/body/eval_jaxpr/all_to_all | solution.py:77
  78.4 0.2 fusion.56
  78.6 10.4 %all-to-all-done = bf16[128,1,8,128]{3,2,1,0:T(8,128)(2,1)S(1)} async-done(((bf16[128,1,8,128]{3,2,1,0:T(8,128)(2,1)}), bf16[128,1,8,128]{3,2,1,0:T(8,128)(2,1)S(1)}, u32[]{:S(2)}, u32[]{:S(2)}) %all-to-all-start) | async-done | bytes 262176 | tf_op jit(solution)/shard_map/while/body/eval_jaxpr/all_to_all | solution.py:77
  89.1 0.2 multiply_subtract_fusion.2
  89.3 0.1 fusion.53
  89.5 0.7 gather_fusion.1
  90.2 6.5 %gather_fusion = bf16[128,128,128]{2,1,0:T(8,128)(2,1)} fusion(bf16[128,2,128,128]{3,2,1,0:T(8,128)(2,1)} %get-tuple-element.546, s32[128]{0:T(128)S(1)} %or_bitcast_fusion.2), kind=kCustom, calls=%fused_computation.2.clone.clone.1 | custom fusion | bytes 8389632 | tf_op jit(solution)/shard_map/while/body/eval_jaxpr/jit(take_along_axis)/gather | solution.py:72
  96.7 4.2 %fusion.55 = bf16[128,1,8,128]{3,2,1,0:T(8,128)(2,1)} fusion(bf16[128,128,128]{2,1,0:T(8,128)(2,1)} %gather_fusion, pred[128]{0:T(512)(128)(4,1)S(1)} %get-tuple-element.506, bf16[128,8,128]{2,1,0:T(8,128)(2,1)S(1)} %gather_fusion.1, pred[128]{0:T(512)(128)(4,1)S(1)} %get-tuple-element.508), kind=kOutput, calls=%fused_computation.11.clone.1 | convolution fusion | flops 35913728 | bytes 4718848 | tf_op jit(solution)/shard_map/while/body/eval_jaxpr/tcrn,tcnm->tcrm/dot_general | solution.py:74
  100.8 4.6 %all-to-all-start = ((bf16[128,1,8,128]{3,2,1,0:T(8,128)(2,1)}), bf16[128,1,8,128]{3,2,1,0:T(8,128)(2,1)S(1)}, u32[]{:S(2)}, u32[]{:S(2)}) async-start(bf16[128,1,8,128]{3,2,1,0:T(8,128)(2,1)} %fusion.55), calls=%async_computation | async-start | bytes 524288 | tf_op jit(solution)/shard_map/while/body/eval_jaxpr/all_to_all | solution.py:77
  105.5 0.2 fusion.56
  105.7 10.4 %all-to-all-done = bf16[128,1,8,128]{3,2,1,0:T(8,128)(2,1)S(1)} async-done(((bf16[128,1,8,128]{3,2,1,0:T(8,128)(2,1)}), bf16[128,1,8,128]{3,2,1,0:T(8,128)(2,1)S(1)}, u32[]{:S(2)}, u32[]{:S(2)}) %all-to-all-start) | async-done | bytes 262176 | tf_op jit(solution)/shard_map/while/body/eval_jaxpr/all_to_all | solution.py:77
  116.1 0.2 multiply_subtract_fusion.2
  116.4 0.1 fusion.53
  116.6 0.7 gather_fusion.1
  117.3 6.5 %gather_fusion = bf16[128,128,128]{2,1,0:T(8,128)(2,1)} fusion(bf16[128,2,128,128]{3,2,1,0:T(8,128)(2,1)} %get-tuple-element.546, s32[128]{0:T(128)S(1)} %or_bitcast_fusion.2), kind=kCustom, calls=%fused_computation.2.clone.clone.1 | custom fusion | bytes 8389632 | tf_op jit(solution)/shard_map/while/body/eval_jaxpr/jit(take_along_axis)/gather | solution.py:72
  123.7 4.2 %fusion.55 = bf16[128,1,8,128]{3,2,1,0:T(8,128)(2,1)} fusion(bf16[128,128,128]{2,1,0:T(8,128)(2,1)} %gather_fusion, pred[128]{0:T(512)(128)(4,1)S(1)} %get-tuple-element.506, bf16[128,8,128]{2,1,0:T(8,128)(2,1)S(1)} %gather_fusion.1, pred[128]{0:T(512)(128)(4,1)S(1)} %get-tuple-element.508), kind=kOutput, calls=%fused_computation.11.clone.1 | convolution fusion | flops 35913728 | bytes 4718848 | tf_op jit(solution)/shard_map/while/body/eval_jaxpr/tcrn,tcnm->tcrm/dot_general | solution.py:74
  127.9 4.6 %all-to-all-start = ((bf16[128,1,8,128]{3,2,1,0:T(8,128)(2,1)}), bf16[128,1,8,128]{3,2,1,0:T(8,128)(2,1)S(1)}, u32[]{:S(2)}, u32[]{:S(2)}) async-start(bf16[128,1,8,128]{3,2,1,0:T(8,128)(2,1)} %fusion.55), calls=%async_computation | async-start | bytes 524288 | tf_op jit(solution)/shard_map/while/body/eval_jaxpr/all_to_all | solution.py:77
  132.5 0.2 fusion.56
  132.7 10.4 %all-to-all-done = bf16[128,1,8,128]{3,2,1,0:T(8,128)(2,1)S(1)} async-done(((bf16[128,1,8,128]{3,2,1,0:T(8,128)(2,1)}), bf16[128,1,8,128]{3,2,1,0:T(8,128)(2,1)S(1)}, u32[]{:S(2)}, u32[]{:S(2)}) %all-to-all-start) | async-done | bytes 262176 | tf_op jit(solution)/shard_map/while/body/eval_jaxpr/all_to_all | solution.py:77
  143.2 0.2 multiply_subtract_fusion.2
  143.5 0.1 fusion.53
  143.7 0.7 gather_fusion.1
  144.4 6.5 %gather_fusion = bf16[128,128,128]{2,1,0:T(8,128)(2,1)} fusion(bf16[128,2,128,128]{3,2,1,0:T(8,128)(2,1)} %get-tuple-element.546, s32[128]{0:T(128)S(1)} %or_bitcast_fusion.2), kind=kCustom, calls=%fused_computation.2.clone.clone.1 | custom fusion | bytes 8389632 | tf_op jit(solution)/shard_map/while/body/eval_jaxpr/jit(take_along_axis)/gather | solution.py:72
  150.8 4.2 %fusion.55 = bf16[128,1,8,128]{3,2,1,0:T(8,128)(2,1)} fusion(bf16[128,128,128]{2,1,0:T(8,128)(2,1)} %gather_fusion, pred[128]{0:T(512)(128)(4,1)S(1)} %get-tuple-element.506, bf16[128,8,128]{2,1,0:T(8,128)(2,1)S(1)} %gather_fusion.1, pred[128]{0:T(512)(128)(4,1)S(1)} %get-tuple-element.508), kind=kOutput, calls=%fused_computation.11.clone.1 | convolution fusion | flops 35913728 | bytes 4718848 | tf_op jit(solution)/shard_map/while/body/eval_jaxpr/tcrn,tcnm->tcrm/dot_general | solution.py:74
  155.0 4.6 %all-to-all-start = ((bf16[128,1,8,128]{3,2,1,0:T(8,128)(2,1)}), bf16[128,1,8,128]{3,2,1,0:T(8,128)(2,1)S(1)}, u32[]{:S(2)}, u32[]{:S(2)}) async-start(bf16[128,1,8,128]{3,2,1,0:T(8,128)(2,1)} %fusion.55), calls=%async_computation | async-start | bytes 524288 | tf_op jit(solution)/shard_map/while/body/eval_jaxpr/all_to_all | solution.py:77
  159.6 0.2 fusion.56
  159.8 10.4 %all-to-all-done = bf16[128,1,8,128]{3,2,1,0:T(8,128)(2,1)S(1)} async-done(((bf16[128,1,8,128]{3,2,1,0:T(8,128)(2,1)}), bf16[128,1,8,128]{3,2,1,0:T(8,128)(2,1)S(1)}, u32[]{:S(2)}, u32[]{:S(2)}) %all-to-all-start) | async-done | bytes 262176 | tf_op jit(solution)/shard_map/while/body/eval_jaxpr/all_to_all | solution.py:77
  170.3 0.2 multiply_subtract_fusion.2
  170.5 0.7 reshape.391
  171.2 3.2 %all-to-all-start.2 = ((f32[4,1,320]{2,1,0:T(1,128)}), f32[4,1,320]{2,1,0:T(1,128)S(1)}, u32[]{:S(2)}, u32[]{:S(2)}) async-start(f32[4,1,320]{2,1,0:T(1,128)} %reshape.391), calls=%async_computation.2 | async-start | bytes 12288 | tf_op jit(solution)/shard_map/all_to_all | solution.py:14
  174.4 0.7 copy.82
  175.2 0.7 copy.83
  175.9 3.8 %all-to-all-done.2 = f32[4,1,320]{2,1,0:T(1,128)S(1)} async-done(((f32[4,1,320]{2,1,0:T(1,128)}), f32[4,1,320]{2,1,0:T(1,128)S(1)}, u32[]{:S(2)}, u32[]{:S(2)}) %all-to-all-start.2) | async-done | bytes 5152 | tf_op jit(solution)/shard_map/all_to_all | solution.py:14
  179.7 0.5 broadcast.389
  180.2 0.7 reduce.2
  180.9 0.1 reshape.392
  181.0 0.6 multiply_bitcast_fusion
  (79 shorter events, 0.7 us)
Async XLA Ops:
  0.6 7.3 %copy-start.6 = (s32[1,128,2]{1,2,0:T(2,128)S(1)}, s32[1,128,2]{1,2,0:T(2,128)}, u32[]{:S(2)}) copy-start(s32[1,128,2]{1,2,0:T(2,128)} %param.22) | copy-start | bytes 3076
  2.2 11.5 %copy-start.5 = (s32[5,1,128]{2,1,0:T(1,128)S(1)}, s32[5,1,128]{2,1,0:T(1,128)}, u32[]{:S(2)}) copy-start(s32[5,1,128]{2,1,0:T(1,128)} %param.25) | copy-start | bytes 7684
  2.2 11.6 %copy-start.4 = (s32[5,1,128,1]{2,3,1,0:T(1,128)S(1)}, s32[5,1,128,1]{2,3,1,0:T(1,128)}, u32[]{:S(2)}) copy-start(s32[5,1,128,1]{2,3,1,0:T(1,128)} %param.24) | copy-start | bytes 7684
  2.2 23.5 %copy-start.2 = (f32[8,4096]{1,0:T(8,128)S(1)}, f32[8,4096]{1,0:T(8,128)}, u32[]{:S(2)}) copy-start(f32[8,4096]{1,0:T(8,128)} %param.17) | copy-start | bytes 393220
  2.3 23.5 %copy-start.3 = (f32[8,4096]{1,0:T(8,128)S(1)}, f32[8,4096]{1,0:T(8,128)}, u32[]{:S(2)}) copy-start(f32[8,4096]{1,0:T(8,128)} %param.16) | copy-start | bytes 393220
  2.3 23.6 %copy-start.1 = (f32[8,4096]{1,0:T(8,128)S(1)}, f32[8,4096]{1,0:T(8,128)}, u32[]{:S(2)}) copy-start(f32[8,4096]{1,0:T(8,128)} %param.15) | copy-start | bytes 393220
  2.3 32.8 %copy-start = (f32[4096]{0:T(1024)S(1)}, f32[4096]{0:T(1024)}, u32[]{:S(2)}) copy-start(f32[4096]{0:T(1024)} %param.19) | copy-start | bytes 49156
  2.3 32.8 %copy-start.7 = (f32[4096]{0:T(1024)S(1)}, f32[4096]{0:T(1024)}, u32[]{:S(2)}) copy-start(f32[4096]{0:T(1024)} %param.18) | copy-start | bytes 49156
  2.3 32.8 %copy-start.8 = (s32[32]{0:T(128)S(1)}, s32[32]{0:T(128)}, u32[]{:S(2)}) copy-start(s32[32]{0:T(128)} %param.23) | copy-start | bytes 388
  14.6 20.4 %all-to-all-start.1 = ((s32[5,128,1]{0,2,1:T(1,128)}), s32[5,128,1]{0,2,1:T(1,128)S(1)}, u32[]{:S(2)}, u32[]{:S(2)}) async-start(s32[5,128,1]{0,2,1:T(1,128)} %copy.58), calls=%async_computation.1 | async-start | bytes 131072 | tf_op jit(solution)/shard_map/all_to_all | solution.py:52
  46.7 15.3 %all-to-all-start = ((bf16[128,1,8,128]{3,2,1,0:T(8,128)(2,1)}), bf16[128,1,8,128]{3,2,1,0:T(8,128)(2,1)S(1)}, u32[]{:S(2)}, u32[]{:S(2)}) async-start(bf16[128,1,8,128]{3,2,1,0:T(8,128)(2,1)} %fusion.55), calls=%async_computation | async-start | bytes 524288 | tf_op jit(solution)/shard_map/while/body/eval_jaxpr/all_to_all | solution.py:77
  73.8 15.3 %all-to-all-start = ((bf16[128,1,8,128]{3,2,1,0:T(8,128)(2,1)}), bf16[128,1,8,128]{3,2,1,0:T(8,128)(2,1)S(1)}, u32[]{:S(2)}, u32[]{:S(2)}) async-start(bf16[128,1,8,128]{3,2,1,0:T(8,128)(2,1)} %fusion.55), calls=%async_computation | async-start | bytes 524288 | tf_op jit(solution)/shard_map/while/body/eval_jaxpr/all_to_all | solution.py:77
  100.8 15.3 %all-to-all-start = ((bf16[128,1,8,128]{3,2,1,0:T(8,128)(2,1)}), bf16[128,1,8,128]{3,2,1,0:T(8,128)(2,1)S(1)}, u32[]{:S(2)}, u32[]{:S(2)}) async-start(bf16[128,1,8,128]{3,2,1,0:T(8,128)(2,1)} %fusion.55), calls=%async_computation | async-start | bytes 524288 | tf_op jit(solution)/shard_map/while/body/eval_jaxpr/all_to_all | solution.py:77
  127.9 15.3 %all-to-all-start = ((bf16[128,1,8,128]{3,2,1,0:T(8,128)(2,1)}), bf16[128,1,8,128]{3,2,1,0:T(8,128)(2,1)S(1)}, u32[]{:S(2)}, u32[]{:S(2)}) async-start(bf16[128,1,8,128]{3,2,1,0:T(8,128)(2,1)} %fusion.55), calls=%async_computation | async-start | bytes 524288 | tf_op jit(solution)/shard_map/while/body/eval_jaxpr/all_to_all | solution.py:77
  155.0 15.3 %all-to-all-start = ((bf16[128,1,8,128]{3,2,1,0:T(8,128)(2,1)}), bf16[128,1,8,128]{3,2,1,0:T(8,128)(2,1)S(1)}, u32[]{:S(2)}, u32[]{:S(2)}) async-start(bf16[128,1,8,128]{3,2,1,0:T(8,128)(2,1)} %fusion.55), calls=%async_computation | async-start | bytes 524288 | tf_op jit(solution)/shard_map/while/body/eval_jaxpr/all_to_all | solution.py:77
  171.2 8.5 %all-to-all-start.2 = ((f32[4,1,320]{2,1,0:T(1,128)}), f32[4,1,320]{2,1,0:T(1,128)S(1)}, u32[]{:S(2)}, u32[]{:S(2)}) async-start(f32[4,1,320]{2,1,0:T(1,128)} %reshape.391), calls=%async_computation.2 | async-start | bytes 12288 | tf_op jit(solution)/shard_map/all_to_all | solution.py:14
where the time goes:
time: 182 us
  waiting for transfers between devices  65.1 us (36%)
  local copies, waits for them, and re-layouts  51.9 us (29%)
  starting transfers between devices  37.5 us (21%)
  matrix products  22.6 us (12%)
  other arithmetic  3.01 us (2%)
    all_to_all x5, waiting for transfers between devices, advance(): lax.all_to_all(outgoing, ('area', 'local'), split_axis=0, concat_axis=0,...  52.2 us
    gather x5, local copies, waits for them, and re-layouts, advance(): picked = jnp.take_along_axis(tile_table, chosen[:, :, None, None], axis=1)  32.3 us
    all_to_all x5, starting transfers between devices, advance(): lax.all_to_all(outgoing, ('area', 'local'), split_axis=0, concat_axis=0,...  23.1 us
    dot_general x5, matrix products, advance(): jnp.einsum('tcrn,tcnm->tcrm', senders, picked, preferred_element_type=jnp...  20.8 us
    all_to_all x1, starting transfers between devices, shards(): lax.all_to_all(dst_ids, ('area', 'local'), split_axis=1, concat_axis=1, t...  11.2 us
    all_to_all x1, waiting for transfers between devices, shards(): lax.all_to_all(dst_ids, ('area', 'local'), split_axis=1, concat_axis=1, t...  9.13 us
    gather x2, local copies, waits for them, and re-layouts, shards(): jnp.take_along_axis(jnp.broadcast_to(tile_dst[0][None], table_shape), rou...  5.64 us
    gather x2, local copies, waits for them, and re-layouts, shards(): jnp.take_along_axis(jnp.broadcast_to(tile_src[0][None], table_shape), rou...  5.64 us
  transfers between devices with their start and end apart: 7, of which 7 were waited for; matrix products, arithmetic and copies ran while one was open for 1% of the time, Pallas kernels for 0%

commit v1 on v0

--- a/solution.py
+++ b/solution.py
@@ -49,9 +49,10 @@
         jnp.broadcast_to(tile_dst[0][None], table_shape), routes, axis=2
     )
     dst_ids = jnp.where(slot_valid, dst_blocks, -1)
-    arrived_ids = lax.all_to_all(
-        dst_ids, ("area", "local"), split_axis=1, concat_axis=1, tiled=True
-    )
+    size = lax.axis_size(("area", "local"))
+    pieces = jnp.stack(jnp.split(dst_ids, size, axis=1), axis=0)
+    pieces = lax.all_to_all(pieces, ("area", "local"), split_axis=0, concat_axis=0)
+    arrived_ids = jnp.concatenate(pieces, axis=1)
     state_shape = (trial_count, blk_count, block_width)
     volts = potential.reshape(state_shape)
     syn_cur = current.reshape(state_shape)

time: 182 us -> 260 us (1.43)
  local copies, waits for them, and re-layouts: 51.9 us -> 130 us
    unnamed x25 -> x151, local copies, waits for them, and re-layouts: 2.42 us -> 67.3 us
    split x0 -> x7, local copies, waits for them, and re-layouts: none -> 13.1 us  [shards(): pieces = jnp.stack(jnp.split(dst_ids, size, axis=1), axis=0)]
where the time goes in v1:
time: 260 us; the launch traced here: 259 us
  local copies, waits for them, and re-layouts  130 us (50%)
  waiting for transfers between devices  65.1 us (25%)
  starting transfers between devices  37.5 us (14%)
  matrix products  22.6 us (9%)
  other arithmetic  3.01 us (1%)
    unnamed x151, local copies, waits for them, and re-layouts  67.3 us
    all_to_all x5, waiting for transfers between devices, advance(): lax.all_to_all(outgoing, ('area', 'local'), split_axis=0, concat_axis=0,...  52.2 us
    gather x5, local copies, waits for them, and re-layouts, advance(): picked = jnp.take_along_axis(tile_table, chosen[:, :, None, None], axis=1)  32.2 us
    all_to_all x5, starting transfers between devices, advance(): lax.all_to_all(outgoing, ('area', 'local'), split_axis=0, concat_axis=0,...  23.1 us
    dot_general x5, matrix products, advance(): jnp.einsum('tcrn,tcnm->tcrm', senders, picked, preferred_element_type=jnp...  20.7 us
    split x7, local copies, waits for them, and re-layouts, shards(): pieces = jnp.stack(jnp.split(dst_ids, size, axis=1), axis=0)  13.1 us
    all_to_all x1, starting transfers between devices, shards(): lax.all_to_all(pieces, ('area', 'local'), split_axis=0, concat_axis=0)  11.2 us
    all_to_all x1, waiting for transfers between devices, shards(): lax.all_to_all(pieces, ('area', 'local'), split_axis=0, concat_axis=0)  9.13 us
  transfers between devices with their start and end apart: 7, of which 7 were waited for; matrix products, arithmetic and copies ran while one was open for 1% of the time, Pallas kernels for 0%

profile of v1, /device:TPU:0, one launch (start us, length us, event | category | flops | bytes accessed | tf_op | source)
XLA Modules:
  0.0 259.3 jit_solution(2038321351282050173)
XLA Ops:
  0.6 0.7 fusion.37
  1.4 0.8 copy.584
  2.3 5.6 %gather_fusion.2 = s32[640]{0:T(1024)S(1)} fusion(s32[5,128,2]{2,1,0:T(8,128)S(1)} %broadcast_in_dim.74, s32[640]{0:T(1024)S(1)} %bitcast.376), kind=kCustom, calls=%fused_computation.clone | custom fusion | bytes 12800 | tf_op jit(solution)/shard_map/jit(take_along_axis)/gather | solution.py:45
  8.1 5.6 %gather_fusion.3 = s32[640]{0:T(1024)S(1)} fusion(s32[5,128,2]{2,1,0:T(8,128)S(1)} %broadcast_in_dim.76, s32[640]{0:T(1024)S(1)} %bitcast.377), kind=kCustom, calls=%fused_computation.3.clone | custom fusion | bytes 12800 | tf_op jit(solution)/shard_map/jit(take_along_axis)/gather | solution.py:48
  13.8 1.4 slice_reduce_fusion.114
  15.2 1.9 slice_reduce_fusion.95
  17.2 1.9 slice_reduce_fusion.76
  19.1 1.9 slice_reduce_fusion.57
  21.0 1.9 slice_reduce_fusion.38
  22.9 1.9 slice_reduce_fusion.19
  24.8 2.1 slice_reduce_fusion
  26.9 0.5 constant_dynamic-update-slice_fusion.127
  30.0 0.5 constant_dynamic-update-slice_fusion.121
  30.5 0.5 constant_dynamic-update-slice_fusion.120
  31.0 0.5 constant_dynamic-update-slice_fusion.119
  31.5 0.5 constant_dynamic-update-slice_fusion.118
  32.0 0.5 constant_dynamic-update-slice_fusion.117
  32.5 0.5 constant_dynamic-update-slice_fusion.116
  33.0 0.5 constant_dynamic-update-slice_fusion.115
  33.5 0.5 constant_dynamic-update-slice_fusion.114
  34.1 0.5 constant_dynamic-update-slice_fusion.113
  34.6 0.5 constant_dynamic-update-slice_fusion.112
  35.1 0.5 constant_dynamic-update-slice_fusion.111
  35.6 0.5 constant_dynamic-update-slice_fusion.110
  39.7 0.5 constant_dynamic-update-slice_fusion.102
  40.2 0.5 constant_dynamic-update-slice_fusion.101
  40.7 0.5 constant_dynamic-update-slice_fusion.100
  41.2 0.5 constant_dynamic-update-slice_fusion.99
  41.7 0.5 constant_dynamic-update-slice_fusion.98
  92.4 11.2 %all-to-all-start.1 = ((s32[128,5,1,1]{1,3,2,0:T(1,128)}), s32[128,5,1,1]{1,3,2,0:T(1,128)S(1)}, u32[]{:S(2)}, u32[]{:S(2)}) async-start(s32[128,5,1,1]{1,3,2,0:T(1,128)} %constant_dynamic-update-slice_fusion), calls=%async_computation.1 | async-start | bytes 131072 | tf_op jit(solution)/shard_map/all_to_all | solution.py:54
  103.7 9.1 %all-to-all-done.1 = s32[128,5,1,1]{1,3,2,0:T(1,128)S(1)} async-done(((s32[128,5,1,1]{1,3,2,0:T(1,128)}), s32[128,5,1,1]{1,3,2,0:T(1,128)S(1)}, u32[]{:S(2)}, u32[]{:S(2)}) %all-to-all-start.1) | async-done | bytes 2592 | tf_op jit(solution)/shard_map/all_to_all | solution.py:54
  112.9 135.2 %while.20 = (s32[]{:T(128)}, f32[8,32,128]{2,1,0:T(8,128)S(1)}, f32[8,32,128]{2,1,0:T(8,128)S(1)}, f32[5,8,8]{2,1,0:T(8,128)S(1)}, f32[1,32,128]{2,1,0:T(8,128)S...) while((s32[]{:T(128)}, f32[8,32,128]{2,1,0:T(8,128)S(1)}, ...), condition=%wide.region_2.0_spmd.clone, body=%wide.region_0.3_spmd.clone.sunk | while | flops 44994944 | bytes 15770289 | solution.py:94
  113.2 0.7 gather_fusion.1
  113.9 6.4 %gather_fusion = bf16[128,128,128]{2,1,0:T(8,128)(2,1)} fusion(bf16[128,2,128,128]{3,2,1,0:T(8,128)(2,1)} %get-tuple-element.674, s32[128]{0:T(128)S(1)} %or_bitcast_fusion.2), kind=kCustom, calls=%fused_computation.2.clone.clone.1 | custom fusion | bytes 8389632 | tf_op jit(solution)/shard_map/while/body/eval_jaxpr/jit(take_along_axis)/gather | solution.py:73
  120.3 4.1 %fusion.55 = bf16[128,1,8,128]{3,2,1,0:T(8,128)(2,1)} fusion(bf16[128,128,128]{2,1,0:T(8,128)(2,1)} %gather_fusion, pred[128]{0:T(512)(128)(4,1)S(1)} %get-tuple-element.634, bf16[128,8,128]{2,1,0:T(8,128)(2,1)S(1)} %gather_fusion.1, pred[128]{0:T(512)(128)(4,1)S(1)} %get-tuple-element.636), kind=kOutput, calls=%fused_computation.11.clone.1 | convolution fusion | flops 35913728 | bytes 4718848 | tf_op jit(solution)/shard_map/while/body/eval_jaxpr/tcrn,tcnm->tcrm/dot_general | solution.py:75
  124.5 4.6 %all-to-all-start = ((bf16[128,1,8,128]{3,2,1,0:T(8,128)(2,1)}), bf16[128,1,8,128]{3,2,1,0:T(8,128)(2,1)S(1)}, u32[]{:S(2)}, u32[]{:S(2)}) async-start(bf16[128,1,8,128]{3,2,1,0:T(8,128)(2,1)} %fusion.55), calls=%async_computation | async-start | bytes 524288 | tf_op jit(solution)/shard_map/while/body/eval_jaxpr/all_to_all | solution.py:78
  129.3 10.4 %all-to-all-done = bf16[128,1,8,128]{3,2,1,0:T(8,128)(2,1)S(1)} async-done(((bf16[128,1,8,128]{3,2,1,0:T(8,128)(2,1)}), bf16[128,1,8,128]{3,2,1,0:T(8,128)(2,1)S(1)}, u32[]{:S(2)}, u32[]{:S(2)}) %all-to-all-start) | async-done | bytes 262176 | tf_op jit(solution)/shard_map/while/body/eval_jaxpr/all_to_all | solution.py:78
  140.3 0.7 gather_fusion.1
  140.9 6.4 %gather_fusion = bf16[128,128,128]{2,1,0:T(8,128)(2,1)} fusion(bf16[128,2,128,128]{3,2,1,0:T(8,128)(2,1)} %get-tuple-element.674, s32[128]{0:T(128)S(1)} %or_bitcast_fusion.2), kind=kCustom, calls=%fused_computation.2.clone.clone.1 | custom fusion | bytes 8389632 | tf_op jit(solution)/shard_map/while/body/eval_jaxpr/jit(take_along_axis)/gather | solution.py:73
  147.4 4.1 %fusion.55 = bf16[128,1,8,128]{3,2,1,0:T(8,128)(2,1)} fusion(bf16[128,128,128]{2,1,0:T(8,128)(2,1)} %gather_fusion, pred[128]{0:T(512)(128)(4,1)S(1)} %get-tuple-element.634, bf16[128,8,128]{2,1,0:T(8,128)(2,1)S(1)} %gather_fusion.1, pred[128]{0:T(512)(128)(4,1)S(1)} %get-tuple-element.636), kind=kOutput, calls=%fused_computation.11.clone.1 | convolution fusion | flops 35913728 | bytes 4718848 | tf_op jit(solution)/shard_map/while/body/eval_jaxpr/tcrn,tcnm->tcrm/dot_general | solution.py:75
  151.5 4.6 %all-to-all-start = ((bf16[128,1,8,128]{3,2,1,0:T(8,128)(2,1)}), bf16[128,1,8,128]{3,2,1,0:T(8,128)(2,1)S(1)}, u32[]{:S(2)}, u32[]{:S(2)}) async-start(bf16[128,1,8,128]{3,2,1,0:T(8,128)(2,1)} %fusion.55), calls=%async_computation | async-start | bytes 524288 | tf_op jit(solution)/shard_map/while/body/eval_jaxpr/all_to_all | solution.py:78
  156.4 10.4 %all-to-all-done = bf16[128,1,8,128]{3,2,1,0:T(8,128)(2,1)S(1)} async-done(((bf16[128,1,8,128]{3,2,1,0:T(8,128)(2,1)}), bf16[128,1,8,128]{3,2,1,0:T(8,128)(2,1)S(1)}, u32[]{:S(2)}, u32[]{:S(2)}) %all-to-all-start) | async-done | bytes 262176 | tf_op jit(solution)/shard_map/while/body/eval_jaxpr/all_to_all | solution.py:78
  167.3 0.7 gather_fusion.1
  168.0 6.4 %gather_fusion = bf16[128,128,128]{2,1,0:T(8,128)(2,1)} fusion(bf16[128,2,128,128]{3,2,1,0:T(8,128)(2,1)} %get-tuple-element.674, s32[128]{0:T(128)S(1)} %or_bitcast_fusion.2), kind=kCustom, calls=%fused_computation.2.clone.clone.1 | custom fusion | bytes 8389632 | tf_op jit(solution)/shard_map/while/body/eval_jaxpr/jit(take_along_axis)/gather | solution.py:73
  174.4 4.1 %fusion.55 = bf16[128,1,8,128]{3,2,1,0:T(8,128)(2,1)} fusion(bf16[128,128,128]{2,1,0:T(8,128)(2,1)} %gather_fusion, pred[128]{0:T(512)(128)(4,1)S(1)} %get-tuple-element.634, bf16[128,8,128]{2,1,0:T(8,128)(2,1)S(1)} %gather_fusion.1, pred[128]{0:T(512)(128)(4,1)S(1)} %get-tuple-element.636), kind=kOutput, calls=%fused_computation.11.clone.1 | convolution fusion | flops 35913728 | bytes 4718848 | tf_op jit(solution)/shard_map/while/body/eval_jaxpr/tcrn,tcnm->tcrm/dot_general | solution.py:75
  178.6 4.6 %all-to-all-start = ((bf16[128,1,8,128]{3,2,1,0:T(8,128)(2,1)}), bf16[128,1,8,128]{3,2,1,0:T(8,128)(2,1)S(1)}, u32[]{:S(2)}, u32[]{:S(2)}) async-start(bf16[128,1,8,128]{3,2,1,0:T(8,128)(2,1)} %fusion.55), calls=%async_computation | async-start | bytes 524288 | tf_op jit(solution)/shard_map/while/body/eval_jaxpr/all_to_all | solution.py:78
  183.4 10.4 %all-to-all-done = bf16[128,1,8,128]{3,2,1,0:T(8,128)(2,1)S(1)} async-done(((bf16[128,1,8,128]{3,2,1,0:T(8,128)(2,1)}), bf16[128,1,8,128]{3,2,1,0:T(8,128)(2,1)S(1)}, u32[]{:S(2)}, u32[]{:S(2)}) %all-to-all-start) | async-done | bytes 262176 | tf_op jit(solution)/shard_map/while/body/eval_jaxpr/all_to_all | solution.py:78
  194.3 0.7 gather_fusion.1
  195.0 6.4 %gather_fusion = bf16[128,128,128]{2,1,0:T(8,128)(2,1)} fusion(bf16[128,2,128,128]{3,2,1,0:T(8,128)(2,1)} %get-tuple-element.674, s32[128]{0:T(128)S(1)} %or_bitcast_fusion.2), kind=kCustom, calls=%fused_computation.2.clone.clone.1 | custom fusion | bytes 8389632 | tf_op jit(solution)/shard_map/while/body/eval_jaxpr/jit(take_along_axis)/gather | solution.py:73
  201.4 4.1 %fusion.55 = bf16[128,1,8,128]{3,2,1,0:T(8,128)(2,1)} fusion(bf16[128,128,128]{2,1,0:T(8,128)(2,1)} %gather_fusion, pred[128]{0:T(512)(128)(4,1)S(1)} %get-tuple-element.634, bf16[128,8,128]{2,1,0:T(8,128)(2,1)S(1)} %gather_fusion.1, pred[128]{0:T(512)(128)(4,1)S(1)} %get-tuple-element.636), kind=kOutput, calls=%fused_computation.11.clone.1 | convolution fusion | flops 35913728 | bytes 4718848 | tf_op jit(solution)/shard_map/while/body/eval_jaxpr/tcrn,tcnm->tcrm/dot_general | solution.py:75
  205.6 4.6 %all-to-all-start = ((bf16[128,1,8,128]{3,2,1,0:T(8,128)(2,1)}), bf16[128,1,8,128]{3,2,1,0:T(8,128)(2,1)S(1)}, u32[]{:S(2)}, u32[]{:S(2)}) async-start(bf16[128,1,8,128]{3,2,1,0:T(8,128)(2,1)} %fusion.55), calls=%async_computation | async-start | bytes 524288 | tf_op jit(solution)/shard_map/while/body/eval_jaxpr/all_to_all | solution.py:78
  210.4 10.4 %all-to-all-done = bf16[128,1,8,128]{3,2,1,0:T(8,128)(2,1)S(1)} async-done(((bf16[128,1,8,128]{3,2,1,0:T(8,128)(2,1)}), bf16[128,1,8,128]{3,2,1,0:T(8,128)(2,1)S(1)}, u32[]{:S(2)}, u32[]{:S(2)}) %all-to-all-start) | async-done | bytes 262176 | tf_op jit(solution)/shard_map/while/body/eval_jaxpr/all_to_all | solution.py:78
  221.3 0.7 gather_fusion.1
  222.0 6.4 %gather_fusion = bf16[128,128,128]{2,1,0:T(8,128)(2,1)} fusion(bf16[128,2,128,128]{3,2,1,0:T(8,128)(2,1)} %get-tuple-element.674, s32[128]{0:T(128)S(1)} %or_bitcast_fusion.2), kind=kCustom, calls=%fused_computation.2.clone.clone.1 | custom fusion | bytes 8389632 | tf_op jit(solution)/shard_map/while/body/eval_jaxpr/jit(take_along_axis)/gather | solution.py:73
  228.5 4.1 %fusion.55 = bf16[128,1,8,128]{3,2,1,0:T(8,128)(2,1)} fusion(bf16[128,128,128]{2,1,0:T(8,128)(2,1)} %gather_fusion, pred[128]{0:T(512)(128)(4,1)S(1)} %get-tuple-element.634, bf16[128,8,128]{2,1,0:T(8,128)(2,1)S(1)} %gather_fusion.1, pred[128]{0:T(512)(128)(4,1)S(1)} %get-tuple-element.636), kind=kOutput, calls=%fused_computation.11.clone.1 | convolution fusion | flops 35913728 | bytes 4718848 | tf_op jit(solution)/shard_map/while/body/eval_jaxpr/tcrn,tcnm->tcrm/dot_general | solution.py:75
  232.6 4.6 %all-to-all-start = ((bf16[128,1,8,128]{3,2,1,0:T(8,128)(2,1)}), bf16[128,1,8,128]{3,2,1,0:T(8,128)(2,1)S(1)}, u32[]{:S(2)}, u32[]{:S(2)}) async-start(bf16[128,1,8,128]{3,2,1,0:T(8,128)(2,1)} %fusion.55), calls=%async_computation | async-start | bytes 524288 | tf_op jit(solution)/shard_map/while/body/eval_jaxpr/all_to_all | solution.py:78
  237.5 10.4 %all-to-all-done = bf16[128,1,8,128]{3,2,1,0:T(8,128)(2,1)S(1)} async-done(((bf16[128,1,8,128]{3,2,1,0:T(8,128)(2,1)}), bf16[128,1,8,128]{3,2,1,0:T(8,128)(2,1)S(1)}, u32[]{:S(2)}, u32[]{:S(2)}) %all-to-all-start) | async-done | bytes 262176 | tf_op jit(solution)/shard_map/while/body/eval_jaxpr/all_to_all | solution.py:78
  248.1 0.7 reshape.527
  248.8 3.2 %all-to-all-start.2 = ((f32[4,1,320]{2,1,0:T(1,128)}), f32[4,1,320]{2,1,0:T(1,128)S(1)}, u32[]{:S(2)}, u32[]{:S(2)}) async-start(f32[4,1,320]{2,1,0:T(1,128)} %reshape.527), calls=%async_computation.2 | async-start | bytes 12288 | tf_op jit(solution)/shard_map/all_to_all | solution.py:14
  252.1 0.7 copy.611
  252.8 0.7 copy.612
  253.5 3.8 %all-to-all-done.2 = f32[4,1,320]{2,1,0:T(1,128)S(1)} async-done(((f32[4,1,320]{2,1,0:T(1,128)}), f32[4,1,320]{2,1,0:T(1,128)S(1)}, u32[]{:S(2)}, u32[]{:S(2)}) %all-to-all-start.2) | async-done | bytes 5152 | tf_op jit(solution)/shard_map/all_to_all | solution.py:14
  257.8 0.7 reduce.258
  258.6 0.6 multiply_bitcast_fusion
  (213 shorter events, 60.3 us)
Async XLA Ops:
  0.6 7.3 %copy-start.6 = (s32[1,128,2]{1,2,0:T(2,128)S(1)}, s32[1,128,2]{1,2,0:T(2,128)}, u32[]{:S(2)}) copy-start(s32[1,128,2]{1,2,0:T(2,128)} %param.22) | copy-start | bytes 3076
  2.2 11.5 %copy-start.5 = (s32[5,1,128]{2,1,0:T(1,128)S(1)}, s32[5,1,128]{2,1,0:T(1,128)}, u32[]{:S(2)}) copy-start(s32[5,1,128]{2,1,0:T(1,128)} %param.25) | copy-start | bytes 7684
  2.2 11.6 %copy-start.4 = (s32[5,1,128,1]{2,3,1,0:T(1,128)S(1)}, s32[5,1,128,1]{2,3,1,0:T(1,128)}, u32[]{:S(2)}) copy-start(s32[5,1,128,1]{2,3,1,0:T(1,128)} %param.24) | copy-start | bytes 7684
  2.2 101.3 %copy-start.2 = (f32[8,4096]{1,0:T(8,128)S(1)}, f32[8,4096]{1,0:T(8,128)}, u32[]{:S(2)}) copy-start(f32[8,4096]{1,0:T(8,128)} %param.17) | copy-start | bytes 393220
  2.3 101.3 %copy-start.3 = (f32[8,4096]{1,0:T(8,128)S(1)}, f32[8,4096]{1,0:T(8,128)}, u32[]{:S(2)}) copy-start(f32[8,4096]{1,0:T(8,128)} %param.16) | copy-start | bytes 393220
  7.9 95.7 %copy-start.1 = (f32[8,4096]{1,0:T(8,128)S(1)}, f32[8,4096]{1,0:T(8,128)}, u32[]{:S(2)}) copy-start(f32[8,4096]{1,0:T(8,128)} %param.15) | copy-start | bytes 393220
  7.9 105.0 %copy-start = (f32[4096]{0:T(1024)S(1)}, f32[4096]{0:T(1024)}, u32[]{:S(2)}) copy-start(f32[4096]{0:T(1024)} %param.19) | copy-start | bytes 49156
  7.9 105.0 %copy-start.7 = (f32[4096]{0:T(1024)S(1)}, f32[4096]{0:T(1024)}, u32[]{:S(2)}) copy-start(f32[4096]{0:T(1024)} %param.18) | copy-start | bytes 49156
  7.9 105.0 %copy-start.8 = (s32[32]{0:T(128)S(1)}, s32[32]{0:T(128)}, u32[]{:S(2)}) copy-start(s32[32]{0:T(128)} %param.23) | copy-start | bytes 388
  92.4 20.4 %all-to-all-start.1 = ((s32[128,5,1,1]{1,3,2,0:T(1,128)}), s32[128,5,1,1]{1,3,2,0:T(1,128)S(1)}, u32[]{:S(2)}, u32[]{:S(2)}) async-start(s32[128,5,1,1]{1,3,2,0:T(1,128)} %constant_dynamic-update-slice_fusion), calls=%async_computation.1 | async-start | bytes 131072 | tf_op jit(solution)/shard_map/all_to_all | solution.py:54
  124.5 15.3 %all-to-all-start = ((bf16[128,1,8,128]{3,2,1,0:T(8,128)(2,1)}), bf16[128,1,8,128]{3,2,1,0:T(8,128)(2,1)S(1)}, u32[]{:S(2)}, u32[]{:S(2)}) async-start(bf16[128,1,8,128]{3,2,1,0:T(8,128)(2,1)} %fusion.55), calls=%async_computation | async-start | bytes 524288 | tf_op jit(solution)/shard_map/while/body/eval_jaxpr/all_to_all | solution.py:78
  151.5 15.3 %all-to-all-start = ((bf16[128,1,8,128]{3,2,1,0:T(8,128)(2,1)}), bf16[128,1,8,128]{3,2,1,0:T(8,128)(2,1)S(1)}, u32[]{:S(2)}, u32[]{:S(2)}) async-start(bf16[128,1,8,128]{3,2,1,0:T(8,128)(2,1)} %fusion.55), calls=%async_computation | async-start | bytes 524288 | tf_op jit(solution)/shard_map/while/body/eval_jaxpr/all_to_all | solution.py:78
  178.6 15.3 %all-to-all-start = ((bf16[128,1,8,128]{3,2,1,0:T(8,128)(2,1)}), bf16[128,1,8,128]{3,2,1,0:T(8,128)(2,1)S(1)}, u32[]{:S(2)}, u32[]{:S(2)}) async-start(bf16[128,1,8,128]{3,2,1,0:T(8,128)(2,1)} %fusion.55), calls=%async_computation | async-start | bytes 524288 | tf_op jit(solution)/shard_map/while/body/eval_jaxpr/all_to_all | solution.py:78
  205.6 15.3 %all-to-all-start = ((bf16[128,1,8,128]{3,2,1,0:T(8,128)(2,1)}), bf16[128,1,8,128]{3,2,1,0:T(8,128)(2,1)S(1)}, u32[]{:S(2)}, u32[]{:S(2)}) async-start(bf16[128,1,8,128]{3,2,1,0:T(8,128)(2,1)} %fusion.55), calls=%async_computation | async-start | bytes 524288 | tf_op jit(solution)/shard_map/while/body/eval_jaxpr/all_to_all | solution.py:78
  232.6 15.3 %all-to-all-start = ((bf16[128,1,8,128]{3,2,1,0:T(8,128)(2,1)}), bf16[128,1,8,128]{3,2,1,0:T(8,128)(2,1)S(1)}, u32[]{:S(2)}, u32[]{:S(2)}) async-start(bf16[128,1,8,128]{3,2,1,0:T(8,128)(2,1)} %fusion.55), calls=%async_computation | async-start | bytes 524288 | tf_op jit(solution)/shard_map/while/body/eval_jaxpr/all_to_all | solution.py:78
  248.8 8.5 %all-to-all-start.2 = ((f32[4,1,320]{2,1,0:T(1,128)}), f32[4,1,320]{2,1,0:T(1,128)S(1)}, u32[]{:S(2)}, u32[]{:S(2)}) async-start(f32[4,1,320]{2,1,0:T(1,128)} %reshape.527), calls=%async_computation.2 | async-start | bytes 12288 | tf_op jit(solution)/shard_map/all_to_all | solution.py:14
